TPU v7x, 32 devices: a whole 2x2x4 slice. The times are simulated.
32 devices in a mesh: rep: 2 (over x), seq: 16 (over z, y, core).
Axes of the slice: x: 2, y: 2, z: 4, core: 2. Of those that a mesh axis runs over, the one named last changes fastest.
Arguments:
- queries: bfloat16 [32, 8192], P('rep', 'seq'), parts along dimension 0, may hold values from -8 to 8
- key_pages: bfloat16 [256, 128, 1024], P(('rep', 'seq')), parts along dimension 0, may hold values from -6 to 6
- value_pages: bfloat16 [256, 128, 1024], P(('rep', 'seq')), parts along dimension 0, may hold values from -6 to 6
- page_table: int32 [32, 8], P('rep'), parts along dimension 0, may hold values from -1 to 127, as said below
- lengths: int32 [32], P('rep'), parts along dimension 0, may hold values from 1 to 1024, as said below
Outputs:
- attention_out: bfloat16 [32, 8192], P('rep', 'seq'), parts along dimension 0
- log_norm: float32 [32, 64], P('rep'), parts along dimension 0
There are 2 independent parts, one for each index of `rep`. A program takes and returns all parts, laid end to end along the dimension named above; each array names one. Nothing has to cross between parts.
Inputs may be any that keep to these rules, and one draw needn't show every extreme that they name: `page_table`: entry j of request r is a global slot id (device index along seq times 8 plus the slot on that device) for j < ceil(lengths[r] / 128) and -1 after; no slot id appears twice; exactly 32 slots are in use in all; the slots in use on each device are its first ones, at least one; some device uses all 8; some request uses 8 pages. `lengths`: A request with 8 pages has 1024 tokens.
All inputs are finite; a program needn't handle non-finite values.
Results may differ from a plain program's by a relative error of at most 0.0085.
Values may be sent and summed in bfloat16 or wider, within the bound.
A program may use at most 64 MiB of HBM per device.

v0:
```python
import math

import jax
import jax.numpy as jnp
from jax import lax
from jax.sharding import PartitionSpec as P

QH = 64
KVH = 8
HEAD = 128


floor_value = -1000000000.0


def attend_block(block_index, running, pool_keys, pool_values, pool_req, pool_tok, whole_queries):
    run_max, run_sum, run_out = running
    per_step = 4
    requests = whole_queries.shape[0]
    page_rows = pool_keys.shape[1]
    group_size = QH // KVH
    start_slot = block_index * per_step
    block_keys = lax.dynamic_slice_in_dim(pool_keys, start_slot, per_step, 0).reshape(
        per_step, page_rows, KVH, HEAD
    )
    block_values = lax.dynamic_slice_in_dim(pool_values, start_slot, per_step, 0).reshape(
        per_step, page_rows, KVH, HEAD
    )
    block_req = lax.dynamic_slice_in_dim(pool_req, start_slot, per_step, 0)
    block_tok = lax.dynamic_slice_in_dim(pool_tok, start_slot, per_step, 0)
    block_queries = whole_queries[block_req].reshape(per_step, KVH, group_size, HEAD)
    scores = jnp.einsum(
        "bkgd,btkd->bkgt", block_queries, block_keys, preferred_element_type=jnp.float32
    ) * (1.0 / math.sqrt(HEAD))
    is_valid = jnp.arange(page_rows, dtype=jnp.int32)[None, :] < block_tok[:, None]
    scores = jnp.where(is_valid[:, None, None, :], scores, floor_value)
    page_max = jnp.max(scores, axis=-1)
    weights = jnp.where(is_valid[:, None, None, :], jnp.exp(scores - page_max[..., None]), 0.0)
    page_sum = jnp.sum(weights, axis=-1).reshape(per_step, QH)
    page_out = jnp.einsum(
        "bkgt,btkd->bkgd",
        weights.astype(jnp.bfloat16),
        block_values,
        preferred_element_type=jnp.float32,
    ).reshape(per_step, QH, HEAD)
    page_max = page_max.reshape(per_step, QH)
    belongs = (block_req[:, None] == jnp.arange(requests, dtype=jnp.int32)[None, :]) & (
        block_tok[:, None] > 0
    )
    candidate = jnp.where(belongs[:, :, None], page_max[:, None, :], floor_value)
    new_max = jnp.maximum(run_max, jnp.max(candidate, axis=0))
    keep_scale = jnp.where(run_max > 0.5 * floor_value, jnp.exp(run_max - new_max), 0.0)
    mixing = jnp.where(belongs[:, :, None], jnp.exp(candidate - new_max[None, :, :]), 0.0)
    run_sum = run_sum * keep_scale + jnp.sum(mixing * page_sum[:, None, :], axis=0)
    run_out = run_out * keep_scale[:, :, None] + jnp.einsum(
        "brh,bhd->rhd", mixing, page_out, precision=lax.Precision.HIGHEST
    )
    return (run_max * 0.0 + new_max, run_sum, run_out)


def body(queries, key_pages, value_pages, page_table, lengths):
    slot_count = key_pages.shape[0]
    page_rows = key_pages.shape[1]
    requests, max_pages = page_table.shape
    devices = lax.axis_size("seq")
    my_index = lax.axis_index("seq")
    whole_queries = lax.all_gather(queries, "seq", axis=1, tiled=True)
    entry_ids = page_table.reshape(-1)
    entry_req = jnp.repeat(jnp.arange(requests, dtype=jnp.int32), max_pages)
    entry_tok = jnp.clip(
        lengths[:, None] - jnp.arange(max_pages, dtype=jnp.int32)[None, :] * page_rows, 0, page_rows
    ).reshape(-1)
    entry_dev = jnp.where(entry_ids >= 0, entry_ids // slot_count, -1)
    local_ids = entry_ids - my_index * slot_count
    slot_range = jnp.arange(slot_count, dtype=jnp.int32)
    matches = (entry_dev[None, :] == my_index) & (local_ids[None, :] == slot_range[:, None])
    pool_req = jnp.sum(jnp.where(matches, entry_req[None, :], 0), axis=1)
    pool_tok = jnp.sum(jnp.where(matches, entry_tok[None, :], 0), axis=1)
    per_step = 4
    block_total = slot_count // per_step
    start_state = (
        jnp.full((requests, QH), floor_value, jnp.float32),
        jnp.zeros((requests, QH), jnp.float32),
        jnp.zeros((requests, QH, HEAD), jnp.float32),
    )

    def step_block(block_index, running):
        return attend_block(
            block_index, running, key_pages, value_pages, pool_req, pool_tok, whole_queries
        )

    run_max, run_sum, run_out = lax.fori_loop(0, block_total, step_block, start_state)
    width_dev = QH * HEAD // devices
    col_heads = (my_index * width_dev + jnp.arange(width_dev, dtype=jnp.int32)) // HEAD
    pieces = lax.all_to_all(
        run_out.reshape(requests, QH * HEAD).astype(jnp.bfloat16),
        "seq",
        split_axis=1,
        concat_axis=0,
        tiled=True,
    ).astype(jnp.float32)
    every_max, every_sum = (
        lax.all_gather(run_max[None], "seq", axis=0, tiled=True),
        lax.all_gather(run_sum[None], "seq", axis=0, tiled=True),
    )
    top_max = jnp.max(every_max, axis=0)
    factor = jnp.exp(every_max - top_max[None])
    totals = jnp.sum(every_sum * factor, axis=0)
    col_factor = jnp.take(factor, col_heads, axis=2)
    shares = jnp.sum(pieces.reshape(devices, requests, width_dev) * col_factor, axis=0)
    denominators = jnp.take(totals, col_heads, axis=1)
    attention_out = (shares / denominators).astype(jnp.bfloat16)
    log_norm = top_max + jnp.log(totals)
    return (attention_out, log_norm)


def solution(mesh):
    placed = (
        P("rep", "seq"),
        P(("rep", "seq"), None, None),
        P(("rep", "seq"), None, None),
        P("rep", None),
        P("rep"),
    )
    return jax.shard_map(
        body,
        mesh=mesh,
        in_specs=placed,
        out_specs=(P("rep", "seq"), P("rep", None)),
        check_vma=False,
    )
```

profile of v0, /device:TPU:0, one launch (start us, length us, event | category | flops | bytes accessed | tf_op | source)
XLA Modules:
  0.0 107.3 jit_solution(14557288509468074840)
XLA Ops:
  0.7 0.8 copy.100
  1.6 0.7 subtract_clamp_fusion
  2.5 24.1 %all_gather.9 = bf16[16,8192]{1,0:T(8,128)(2,1)S(1)} all-gather(bf16[16,512]{1,0:T(8,128)(2,1)} %param.7), channel_id=1, replica_groups=mesh['rep'=2,'seq'=16] {'seq'}, dimensions={1}, use_global_device_ids=true | all-gather | bytes 278528 | tf_op jit(solution)/shard_map/all_gather | solution.py:67
  26.7 19.3 %while.18 = (s32[]{:T(128)}, f32[16,64]{0,1:T(8,128)}, f32[16,64]{0,1:T(8,128)}, f32[16,64,128]{2,0,1:T(8,128)}, s32[8]{0:T(128)S(1)}, /*index=5*/s32[8]{0:T(128...) while((s32[]{:T(128)}, f32[16,64]{0,1:T(8,128)}, ...), condition=%wide.region_7.8_spmd.clone, body=%wide.region_2.7_spmd.clone.sunk | while | flops 23809176 | bytes 16661139 | solution.py:92
  26.9 1.8 %constant_dynamic-slice_fusion.3 = (bf16[4,128,1024]{2,1,0:T(8,128)(2,1)S(1)}, bf16[4,128,1024]{2,1,0:T(8,128)(2,1)S(1)}) fusion(bf16[8,128,1024]{2,1,0:T(8,128)(2,1)} %get-tuple-element.401, s32[]{:T(128)S(6)} %select_n.208, bf16[8,128,1024]{2,1,0:T(8,128)(2,1)} %get-tuple-element.400), kind=kLoop, calls=%fused_computation.39.clone.1 | loop fusion | bytes 4194308 | tf_op jit(solution)/shard_map/while/body/eval_jaxpr/dynamic_slice | solution.py:26
  33.5 1.3 %fusion.57 = f32[16,64,128]{2,0,1:T(8,128)S(1)} fusion(f32[16,64,128]{2,0,1:T(8,128)S(1)} %copy-done, f32[16,64]{0,1:T(8,128)S(1)} %get-tuple-element.365, pred[]{:T(512)S(6)} %compare.24, f32[4,64,128]{2,1,0:T(8,128)S(1)} %convolution_bitcast_fusion.3, f32[16,64]{0,1:T(8,128)S(1)} %select_maximum_fusion.2, f32[4,64]{0,1:T(8,128)S(1)} %bitcast.57, ...), kind=kOutput, calls=%fused_computation.4.clone.1 | convolution fusion | flops 6696960 | bytes 1188929 | tf_op jit(solution)/shard_map/while/body/eval_jaxpr/brh,bhd->rhd/dot_general | solution.py:55
  34.8 0.8 copy-done.1
  35.8 1.8 %constant_dynamic-slice_fusion.3 = (bf16[4,128,1024]{2,1,0:T(8,128)(2,1)S(1)}, bf16[4,128,1024]{2,1,0:T(8,128)(2,1)S(1)}) fusion(bf16[8,128,1024]{2,1,0:T(8,128)(2,1)} %get-tuple-element.401, s32[]{:T(128)S(6)} %select_n.208, bf16[8,128,1024]{2,1,0:T(8,128)(2,1)} %get-tuple-element.400), kind=kLoop, calls=%fused_computation.39.clone.1 | loop fusion | bytes 4194308 | tf_op jit(solution)/shard_map/while/body/eval_jaxpr/dynamic_slice | solution.py:26
  41.2 0.8 select_maximum_fusion.2
  42.5 1.4 %fusion.56 = (f32[16,64]{0,1:T(8,128)}, f32[16,64]{0,1:T(8,128)S(1)}, f32[16,64]{0,1:T(8,128)}) fusion(f32[16,64]{0,1:T(8,128)S(1)} %fusion.55, f32[16,64]{0,1:T(8,128)} %get-tuple-element.382, pred[]{:T(512)S(6)} %compare.24, f32[16,64]{0,1:T(8,128)S(1)} %select_reduce_fusion.4, f32[16,64]{0,1:T(8,128)} %get-tuple-element.381), kind=kLoop, calls=%fused_computation.30.clone.1 | loop fusion | flops 10240 | bytes 28673 | tf_op jit(solution)/shard_map/while/body/eval_jaxpr/add | solution.py:54
  43.9 1.3 %fusion.57 = f32[16,64,128]{2,0,1:T(8,128)S(1)} fusion(f32[16,64,128]{2,0,1:T(8,128)S(1)} %copy-done, f32[16,64]{0,1:T(8,128)S(1)} %get-tuple-element.365, pred[]{:T(512)S(6)} %compare.24, f32[4,64,128]{2,1,0:T(8,128)S(1)} %convolution_bitcast_fusion.3, f32[16,64]{0,1:T(8,128)S(1)} %select_maximum_fusion.2, f32[4,64]{0,1:T(8,128)S(1)} %bitcast.57, ...), kind=kOutput, calls=%fused_computation.4.clone.1 | convolution fusion | flops 6696960 | bytes 1188929 | tf_op jit(solution)/shard_map/while/body/eval_jaxpr/brh,bhd->rhd/dot_general | solution.py:55
  45.2 0.8 copy-done.1
  46.0 1.1 %convert_element_type.24 = bf16[16,64,128]{2,0,1:T(8,128)(2,1)S(1)} convert(f32[16,64,128]{2,0,1:T(8,128)} %get-tuple-element.158) | non-fusion elementwise | flops 131072 | bytes 786432 | tf_op jit(solution)/shard_map/convert_element_type | solution.py:96
  47.3 0.8 copy.104
  48.2 3.5 %all-to-all-start = ((bf16[16,16,512]{2,0,1:T(8,128)(2,1)}), bf16[16,16,512]{2,0,1:T(8,128)(2,1)S(1)}, u32[]{:S(2)}, u32[]{:S(2)}) async-start(bf16[16,16,512]{2,0,1:T(8,128)(2,1)} %copy.104), calls=%async_computation | async-start | bytes 524288 | tf_op jit(solution)/shard_map/all_to_all | solution.py:95
  51.7 0.8 copy.106
  52.5 22.0 %all-gather = f32[256,64]{1,0:T(8,128)S(1)} all-gather(f32[16,64]{1,0:T(8,128)S(1)} %copy.106), channel_id=2, replica_groups=mesh['rep'=2,'seq'=16] {'seq'}, dimensions={0}, use_global_device_ids=true | all-gather | bytes 69632 | tf_op jit(solution)/shard_map/all_gather | solution.py:103
  74.6 0.8 copy.108
  75.4 17.8 %all-gather.1 = f32[256,64]{1,0:T(8,128)S(1)} all-gather(f32[16,64]{1,0:T(8,128)S(1)} %copy.108), channel_id=3, replica_groups=mesh['rep'=2,'seq'=16] {'seq'}, dimensions={0}, use_global_device_ids=true | all-gather | bytes 69632 | tf_op jit(solution)/shard_map/all_gather | solution.py:104
  93.6 3.1 %gather_fusion.1 = f32[512,16,16]{2,1,0:T(8,128)} fusion(f32[16,16,64]{1,0,2:T(8,128)S(1)} %copy.107, s32[1024]{0:T(1024)S(1)} %pad_clamp_fusion.1), kind=kCustom, calls=%fused_computation.1 | custom fusion | bytes 1050624 | tf_op jit(solution)/shard_map/jit(_take)/gather | solution.py:109
  96.7 1.0 gather_fusion.2
  98.4 3.0 %copy.105 = f32[16,16,512]{0,1,2:T(8,128)} copy(bf16[16,16,512]{2,0,1:T(8,128)(2,1)S(1)} %all-to-all-done) | data formatting | bytes 786432 | tf_op jit(solution)/shard_map/convert_element_type | solution.py:101
  101.3 5.1 %fusion.26 = f32[16,512]{0,1:T(8,128)S(1)} fusion(f32[16,16,512]{0,1,2:T(8,128)} %copy.105, f32[512,16,16]{2,1,0:T(8,128)} %gather_fusion.1, pred[512]{0:T(512)(128)(4,1)S(1)} %compare_and_fusion), kind=kLoop, calls=%fused_computation.46 | loop fusion | flops 385024 | bytes 1081856 | tf_op jit(solution)/shard_map/reduce_sum | solution.py:110
  106.6 0.7 copy.110
  (62 shorter events, 11.0 us)
Async XLA Ops:
  29.4 4.1 %copy-start = (f32[16,64,128]{2,0,1:T(8,128)S(1)}, f32[16,64,128]{2,0,1:T(8,128)}, u32[]{:S(2)}) copy-start(f32[16,64,128]{2,0,1:T(8,128)} %get-tuple-element.383) | copy-start | bytes 1572868 | tf_op jit(solution)/shard_map/while
  34.8 0.8 copy-start.1
  38.3 5.7 %copy-start = (f32[16,64,128]{2,0,1:T(8,128)S(1)}, f32[16,64,128]{2,0,1:T(8,128)}, u32[]{:S(2)}) copy-start(f32[16,64,128]{2,0,1:T(8,128)} %get-tuple-element.383) | copy-start | bytes 1572868 | tf_op jit(solution)/shard_map/while
  45.2 0.8 copy-start.1
  48.2 50.2 %all-to-all-start = ((bf16[16,16,512]{2,0,1:T(8,128)(2,1)}), bf16[16,16,512]{2,0,1:T(8,128)(2,1)S(1)}, u32[]{:S(2)}, u32[]{:S(2)}) async-start(bf16[16,16,512]{2,0,1:T(8,128)(2,1)} %copy.104), calls=%async_computation | async-start | bytes 524288 | tf_op jit(solution)/shard_map/all_to_all | solution.py:95
where the time goes:
time: 108 us; the launch traced here: 107 us
  blocking collectives  63.9 us (59%)
  local copies, waits for them, and re-layouts  21.4 us (20%)
  other arithmetic  12.6 us (12%)
  matrix products  4.86 us (5%)
  starting transfers between devices  3.53 us (3%)
    all_gather x1, blocking collectives, body(): whole_queries = lax.all_gather(queries, 'seq', axis=1, tiled=True)  24.1 us
    all_gather x1, blocking collectives, body(): lax.all_gather(run_max[None], 'seq', axis=0, tiled=True)  22 us
    all_gather x1, blocking collectives, body(): lax.all_gather(run_sum[None], 'seq', axis=0, tiled=True)  17.8 us
    reduce_sum x1, other arithmetic, body(): jnp.sum(pieces.reshape(devices, requests, width_dev) * col_factor, axis=0)  5.09 us
    dynamic_slice x4, local copies, waits for them, and re-layouts, attend_block(): lax.dynamic_slice_in_dim(pool_values, start_slot, per_step, 0)  4.95 us
    all_to_all x1, starting transfers between devices, body(): lax.all_to_all(run_out.reshape(requests, QH * HEAD).astype(jnp.bfloat16),...  3.53 us
    gather x1, local copies, waits for them, and re-layouts, body(): col_factor = jnp.take(factor, col_heads, axis=2)  3.06 us
    convert_element_type x1, local copies, waits for them, and re-layouts, body(): pieces = lax.all_to_all(run_out.reshape(requests, QH * HEAD).astype(jnp.b...  2.96 us
  transfers between devices with their start and end apart: 1, of which 0 were waited for; matrix products, arithmetic and copies ran while one was open for 6% of the time, Pallas kernels for 0%

commit v1 on v0

--- a/solution.py
+++ b/solution.py
@@ -1,8 +1,11 @@
+import functools
 import math
 
 import jax
 import jax.numpy as jnp
 from jax import lax
+from jax.experimental import pallas as pl
+from jax.experimental.pallas import tpu as pltpu
 from jax.sharding import PartitionSpec as P
 
 QH = 64
@@ -58,7 +61,7 @@
     return (run_max * 0.0 + new_max, run_sum, run_out)
 
 
-def body(queries, key_pages, value_pages, page_table, lengths):
+def generic_body(queries, key_pages, value_pages, page_table, lengths):
     slot_count = key_pages.shape[0]
     page_rows = key_pages.shape[1]
     requests, max_pages = page_table.shape
@@ -114,6 +117,238 @@
     return (attention_out, log_norm)
 
 
+def dot_f32(a, b, contract):
+    return lax.dot_general(
+        a, b, (contract, ((), ())), precision=lax.Precision.HIGHEST, preferred_element_type=jnp.float32
+    )
+
+
+def kernel(
+    n,
+    q_ref,
+    k_hbm,
+    v_hbm,
+    pt_ref,
+    len_ref,
+    out_ref,
+    norm_ref,
+    k_vm,
+    v_vm,
+    q_stage,
+    q_recv,
+    q_rows,
+    o_rows,
+    o_stage,
+    o_recv,
+    st_stage,
+    st_recv,
+    e_rows,
+    k_sem,
+    v_sem,
+    qs_sem,
+    qr_sem,
+    os_sem,
+    or_sem,
+    ss_sem,
+    sr_sem,
+):
+    me = lax.axis_index("seq")
+    slots, page_rows = k_vm.shape[:2]
+    requests, max_pages = pt_ref.shape
+    total_slots = n * slots
+    heads_dev = q_ref.shape[1] // HEAD
+    group = QH // KVH
+
+    k_copies = [pltpu.make_async_copy(k_hbm.at[s], k_vm.at[s], k_sem.at[s]) for s in range(slots)]
+    v_copies = [pltpu.make_async_copy(v_hbm.at[s], v_vm.at[s], v_sem.at[s]) for s in range(slots)]
+    for copy in k_copies + v_copies:
+        copy.start()
+
+    barrier = pltpu.get_barrier_semaphore()
+    for i in range(1, n):
+        pl.semaphore_signal(
+            barrier, inc=1, device_id={"seq": lax.rem(me + i, n)}, device_id_type=pl.DeviceIdType.MESH
+        )
+
+    table = pt_ref[...]
+    row_at = lax.broadcasted_iota(jnp.int32, (requests, 1), 0)
+    len_col = jnp.zeros((requests, 1), jnp.int32)
+    for r in range(requests):
+        len_col = jnp.where(row_at == r, len_ref[r], len_col)
+    slot_lane = lax.broadcasted_iota(jnp.int32, (requests, total_slots), 1)
+    local_lane = lax.broadcasted_iota(jnp.int32, (requests, 128), 1)
+    belongs = jnp.zeros((requests, total_slots), jnp.float32)
+    local_tok = jnp.zeros((requests, 128), jnp.int32)
+    for j in range(max_pages):
+        entry = table[:, j : j + 1]
+        belongs = jnp.where(slot_lane == entry, 1.0, belongs)
+        tok = jnp.clip(len_col - j * page_rows, 0, page_rows)
+        local_tok = jnp.where(local_lane + me * slots == entry, tok, local_tok)
+    local_tok = jnp.max(local_tok, axis=0, keepdims=True)
+
+    belongs_t = jnp.transpose(belongs)
+    picked = jnp.dot(
+        belongs_t.astype(jnp.bfloat16), q_ref[...], preferred_element_type=jnp.float32
+    )
+    picked = jnp.concatenate(
+        [
+            picked[:, h * HEAD : (h + 1) * HEAD].reshape(n, slots, HEAD)
+            for h in range(heads_dev)
+        ],
+        axis=1,
+    )
+    q_stage[...] = picked.astype(jnp.bfloat16)
+    req_col = lax.broadcasted_iota(jnp.int32, (requests, 128), 0).astype(jnp.bfloat16) + 1
+    slot_req = jnp.dot(
+        belongs_t.astype(jnp.bfloat16), req_col, preferred_element_type=jnp.float32
+    )
+
+    pl.semaphore_wait(barrier, n - 1)
+
+    def exchange(stage_of, recv, send_sem, recv_sem):
+        copies = []
+        for i in range(1, n):
+            dst = lax.rem(me + i, n)
+            copies.append(
+                pltpu.make_async_remote_copy(
+                    src_ref=stage_of(dst),
+                    dst_ref=recv.at[me],
+                    send_sem=send_sem.at[i],
+                    recv_sem=recv_sem.at[i],
+                    device_id={"seq": dst},
+                    device_id_type=pl.DeviceIdType.MESH,
+                )
+            )
+            copies[-1].start()
+        return copies
+
+    q_copies = exchange(lambda dst: q_stage.at[dst], q_recv, qs_sem, qr_sem)
+    q_recv[me] = q_stage[me]
+    for copy in q_copies:
+        copy.wait_recv()
+    q_rows[...] = q_recv[...].astype(jnp.float32).reshape(QH * slots, HEAD)
+
+    scale = 1.0 / math.sqrt(HEAD)
+    tok_lane = lax.broadcasted_iota(jnp.int32, (group, page_rows), 1)
+    stat_lane = lax.broadcasted_iota(jnp.int32, (group, 128), 1)
+    tops = [jnp.zeros((group, 128), jnp.float32) for _ in range(KVH)]
+    sums = [jnp.ones((group, 128), jnp.float32) for _ in range(KVH)]
+    weights = {}
+    for s in range(slots):
+        k_copies[s].wait()
+        is_valid = tok_lane < local_tok[:, s : s + 1]
+        for k in range(KVH):
+            q = q_rows[pl.ds(k * group * slots + s, group, stride=slots), :].astype(jnp.bfloat16)
+            scores = lax.dot_general(
+                q,
+                k_vm[s, :, k * HEAD : (k + 1) * HEAD],
+                (((1,), (1,)), ((), ())),
+                preferred_element_type=jnp.float32,
+            )
+            scores = jnp.where(is_valid, scores * scale, floor_value)
+            top = jnp.max(scores, axis=1, keepdims=True)
+            expo = jnp.exp(scores - top)
+            total = jnp.sum(expo, axis=1, keepdims=True)
+            tops[k] = jnp.where(stat_lane == s, top, tops[k])
+            sums[k] = jnp.where(stat_lane == s, total, sums[k])
+            weights[s, k] = (expo.astype(jnp.bfloat16), total)
+    lse = jnp.concatenate(tops, axis=0) + jnp.log(jnp.concatenate(sums, axis=0))
+    lse = jnp.concatenate([lse, jnp.zeros((128 - QH, 128), jnp.float32)], axis=0)
+    st_stage[...] = jnp.transpose(lse)[:slots]
+    st_copies = exchange(lambda dst: st_stage, st_recv, ss_sem, sr_sem)
+    st_recv[me] = st_stage[...]
+
+    for s in range(slots):
+        v_copies[s].wait()
+        for k in range(KVH):
+            expo, total = weights[s, k]
+            part = jnp.dot(
+                expo, v_vm[s, :, k * HEAD : (k + 1) * HEAD], preferred_element_type=jnp.float32
+            )
+            o_rows[pl.ds(k * group * slots + s, group, stride=slots), :] = part / total
+    o_stage[...] = o_rows[...].reshape(n, heads_dev * slots, HEAD).astype(jnp.bfloat16)
+    o_copies = exchange(lambda dst: o_stage.at[dst], o_recv, os_sem, or_sem)
+    o_recv[me] = o_stage[me]
+
+    for copy in st_copies:
+        copy.wait_recv()
+    every = st_recv[...].reshape(total_slots, 128)
+    slot_top = jnp.zeros((total_slots, 128), jnp.float32)
+    req_tops = []
+    for r in range(requests):
+        mine = slot_req == r + 1.0
+        req_top = jnp.max(jnp.where(mine, every, floor_value), axis=0, keepdims=True)
+        slot_top = jnp.where(mine, req_top, slot_top)
+        req_tops.append(req_top)
+    share = jnp.exp(every - slot_top)
+    totals = dot_f32(belongs, share, ((1,), (0,)))
+    log_norm = jnp.concatenate(req_tops, axis=0) + jnp.log(totals)
+    norm_ref[...] = log_norm[:, :QH]
+    e_rows[...] = jnp.transpose(share)
+
+    for copy in o_copies:
+        copy.wait_recv()
+    parts = o_recv[...].astype(jnp.float32)
+    for h in range(heads_dev):
+        mix = belongs * e_rows[pl.ds(me * heads_dev + h, 1), :]
+        value = dot_f32(
+            mix,
+            parts[:, h * slots : (h + 1) * slots, :].reshape(total_slots, HEAD),
+            ((1,), (0,)),
+        )
+        value = value / jnp.sum(mix, axis=1, keepdims=True)
+        out_ref[:, h * HEAD : (h + 1) * HEAD] = value.astype(jnp.bfloat16)
+
+    for copy in q_copies + st_copies + o_copies:
+        copy.wait_send()
+
+
+def fused_body(n, queries, key_pages, value_pages, page_table, lengths):
+    slots, page_rows, width = key_pages.shape
+    requests = queries.shape[0]
+    heads_dev = queries.shape[1] // HEAD
+    vmem = pl.BlockSpec(memory_space=pltpu.VMEM)
+    hbm = pl.BlockSpec(memory_space=pl.ANY)
+    smem = pl.BlockSpec(memory_space=pltpu.SMEM)
+    exchanged = (n, heads_dev * slots, HEAD)
+    return pl.pallas_call(
+        functools.partial(kernel, n),
+        out_shape=(
+            jax.ShapeDtypeStruct(queries.shape, jnp.bfloat16),
+            jax.ShapeDtypeStruct((requests, QH), jnp.float32),
+        ),
+        in_specs=[vmem, hbm, hbm, vmem, smem],
+        out_specs=(vmem, vmem),
+        scratch_shapes=[
+            pltpu.VMEM((slots, page_rows, width), jnp.bfloat16),
+            pltpu.VMEM((slots, page_rows, width), jnp.bfloat16),
+            pltpu.VMEM(exchanged, jnp.bfloat16),
+            pltpu.VMEM(exchanged, jnp.bfloat16),
+            pltpu.VMEM((QH * slots, HEAD), jnp.float32),
+            pltpu.VMEM((QH * slots, HEAD), jnp.float32),
+            pltpu.VMEM(exchanged, jnp.bfloat16),
+            pltpu.VMEM(exchanged, jnp.bfloat16),
+            pltpu.VMEM((slots, 128), jnp.float32),
+            pltpu.VMEM((n, slots, 128), jnp.float32),
+            pltpu.VMEM((128, n * slots), jnp.float32),
+            pltpu.SemaphoreType.DMA((slots,)),
+            pltpu.SemaphoreType.DMA((slots,)),
+        ]
+        + [pltpu.SemaphoreType.DMA((n,))] * 6,
+        compiler_params=pltpu.CompilerParams(collective_id=0, has_side_effects=True),
+    )(queries, key_pages, value_pages, page_table, lengths)
+
+
+def body(queries, key_pages, value_pages, page_table, lengths):
+    n = lax.axis_size("seq")
+    slots, page_rows, _ = key_pages.shape
+    whole_heads = queries.shape[1] % HEAD == 0
+    whole_tiles = slots % 8 == 0 and (n * slots) % 128 == 0 and page_rows % 128 == 0
+    if whole_heads and whole_tiles and slots <= 128:
+        return fused_body(n, queries, key_pages, value_pages, page_table, lengths)
+    return generic_body(queries, key_pages, value_pages, page_table, lengths)
+
+
 def solution(mesh):
     placed = (
         P("rep", "seq"),

time: 108 us -> 28.4 us (0.26)
  blocking collectives: 63.9 us -> 0 us
  Pallas kernels: 0 us -> 23.3 us
  local copies, waits for them, and re-layouts: 21.4 us -> 3.97 us
  other arithmetic: 12.6 us -> 0 us
  matrix products: 4.86 us -> 0 us
  starting transfers between devices: 3.53 us -> 0 us
    all_gather x3 -> x0, blocking collectives: 63.9 us -> none  [the longest x1 24.1 us: body(): whole_queries = lax.all_gather(queries, 'seq', axis=1, tiled=True)]
    pallas_call x0 -> x1, Pallas kernels: none -> 23.3 us  [fused_body(): pl.pallas_call(functools.partial(kernel, n), out_shape=(jax.ShapeDtypeStr...]
    dynamic_slice x6 -> x0, local copies, waits for them, and re-layouts: 6.27 us -> none  [the longest x4 4.95 us: attend_block(): lax.dynamic_slice_in_dim(pool_values, start_slot, per_step, 0)]
    reduce_sum x7 -> x0, other arithmetic: 6.1 us -> none  [the longest x1 5.09 us: body(): jnp.sum(pieces.reshape(devices, requests, width_dev) * col_factor, axis=0)]
    gather x4 -> x0, local copies, waits for them, and re-layouts: 5.31 us -> none  [the longest x1 3.06 us: body(): col_factor = jnp.take(factor, col_heads, axis=2)]
    dot_general x6 -> x0, matrix products: 4.86 us -> none  [the longest x2 2.59 us: attend_block(): jnp.einsum('brh,bhd->rhd', mixing, page_out, precision=lax.Precision.HIGH...]
    convert_element_type x4 -> x0, local copies, waits for them, and re-layouts: 4.03 us -> none  [the longest x1 2.96 us: body(): pieces = lax.all_to_all(run_out.reshape(requests, QH * HEAD).astype(jnp.b...]
    all_to_all x1 -> x0, starting transfers between devices: 3.53 us -> none  [body(): lax.all_to_all(run_out.reshape(requests, QH * HEAD).astype(jnp.bfloat16),...]
  transfers between devices with their start and end apart: 1 -> 0, of which waited for: 0 -> 0; matrix products, arithmetic and copies ran while one was open for 6% -> 0% of each run, Pallas kernels for 0% -> 0%
where the time goes in v1:
time: 28.4 us; the launch traced here: 28 us
  Pallas kernels  23.3 us (82%)
  local copies, waits for them, and re-layouts  3.97 us (14%)
  between operations  0.64 us (2%)
    pallas_call x1, Pallas kernels, fused_body(): pl.pallas_call(functools.partial(kernel, n), out_shape=(jax.ShapeDtypeStr...  23.3 us
    unnamed x3, local copies, waits for them, and re-layouts  3.97 us

profile of v1, /device:TPU:0, one launch (start us, length us, event | category | flops | bytes accessed | tf_op | source)
XLA Modules:
  0.0 28.0 jit_solution(18064486682585288903)
XLA Ops:
  0.6 1.4 %copy.7.pt_ref = s32[16,8]{1,0:T(8,128)} copy(s32[16,8]{0,1:T(8,128)} %param.8) | data formatting | bytes 1024 | tf_op args[3]
  2.0 23.3 %shard_map.68 = (bf16[16,512]{1,0:T(8,128)(2,1)}, f32[16,64]{1,0:T(8,128)}) custom-call(bf16[16,512]{1,0:T(8,128)(2,1)} %q_ref.1, bf16[8,128,1024]{2,1,0:T(8,128)(2,1)} %k_hbm.1, bf16[8,128,1024]{2,1,0:T(8,128)(2,1)} %v_hbm.1, s32[16,8]{1,0:T(8,128)} %copy.7.pt_ref, s32[16]{0:T(128)} %len_ref.1), custom_call_target="tpu_custom_call" | custom-call | tf_op jit(solution)/shard_map/pallas_call | solution.py:314
  25.3 1.3 %copy.10 = bf16[16,512]{1,0:T(8,128)(2,1)} copy(bf16[16,512]{1,0:T(8,128)(2,1)} %get-tuple-element.4) | data formatting | bytes 32768
  26.7 1.3 %copy.11 = f32[16,64]{1,0:T(8,128)} copy(f32[16,64]{1,0:T(8,128)} %get-tuple-element.5) | data formatting | bytes 8192

commit v2 on v1

--- a/solution.py
+++ b/solution.py
@@ -154,7 +154,7 @@
 ):
     me = lax.axis_index("seq")
     slots, page_rows = k_vm.shape[:2]
-    requests, max_pages = pt_ref.shape
+    max_pages, requests = pt_ref.shape
     total_slots = n * slots
     heads_dev = q_ref.shape[1] // HEAD
     group = QH // KVH
@@ -170,7 +170,7 @@
             barrier, inc=1, device_id={"seq": lax.rem(me + i, n)}, device_id_type=pl.DeviceIdType.MESH
         )
 
-    table = pt_ref[...]
+    table = jnp.transpose(pt_ref[...])
     row_at = lax.broadcasted_iota(jnp.int32, (requests, 1), 0)
     len_col = jnp.zeros((requests, 1), jnp.int32)
     for r in range(requests):
@@ -303,6 +303,11 @@
         copy.wait_send()
 
 
+def place(out_in, norm_in, out_ref, norm_ref):
+    out_ref[...] = out_in[...]
+    norm_ref[...] = norm_in[...]
+
+
 def fused_body(n, queries, key_pages, value_pages, page_table, lengths):
     slots, page_rows, width = key_pages.shape
     requests = queries.shape[0]
@@ -311,7 +316,7 @@
     hbm = pl.BlockSpec(memory_space=pl.ANY)
     smem = pl.BlockSpec(memory_space=pltpu.SMEM)
     exchanged = (n, heads_dev * slots, HEAD)
-    return pl.pallas_call(
+    parts = pl.pallas_call(
         functools.partial(kernel, n),
         out_shape=(
             jax.ShapeDtypeStruct(queries.shape, jnp.bfloat16),
@@ -336,7 +341,13 @@
         ]
         + [pltpu.SemaphoreType.DMA((n,))] * 6,
         compiler_params=pltpu.CompilerParams(collective_id=0, has_side_effects=True),
-    )(queries, key_pages, value_pages, page_table, lengths)
+    )(queries, key_pages, value_pages, page_table.T, lengths)
+    return pl.pallas_call(
+        place,
+        out_shape=tuple(jax.ShapeDtypeStruct(a.shape, a.dtype) for a in parts),
+        in_specs=[vmem] * 2,
+        out_specs=(vmem, vmem),
+    )(*parts)
 
 
 def body(queries, key_pages, value_pages, page_table, lengths):

time: 28.4 us -> 25.7 us (0.905)
  local copies, waits for them, and re-layouts: 3.97 us -> 0 us
  Pallas kernels: 23.3 us -> 24.7 us
    unnamed x3 -> x0, local copies, waits for them, and re-layouts: 3.97 us -> none
    pallas_call x0 -> x1, Pallas kernels: none -> 1.33 us  [fused_body(): pl.pallas_call(place, out_shape=tuple((jax.ShapeDtypeStruct(a.shape, a.dt...]
where the time goes in v2:
time: 25.7 us; the launch traced here: 25.3 us
  Pallas kernels  24.7 us (96%)
  between operations  0.64 us (2%)
    pallas_call x1, Pallas kernels, fused_body(): pl.pallas_call(functools.partial(kernel, n), out_shape=(jax.ShapeDtypeStr...  23.4 us
    pallas_call x1, Pallas kernels, fused_body(): pl.pallas_call(place, out_shape=tuple((jax.ShapeDtypeStruct(a.shape, a.dt...  1.33 us

profile of v2, /device:TPU:0, one launch (start us, length us, event | category | flops | bytes accessed | tf_op | source)
XLA Modules:
  0.0 25.3 jit_solution(4143802083148293463)
XLA Ops:
  0.6 23.4 %shard_map.68 = (bf16[16,512]{1,0:T(8,128)(2,1)}, f32[16,64]{1,0:T(8,128)}) custom-call(bf16[16,512]{1,0:T(8,128)(2,1)} %q_ref.1, bf16[8,128,1024]{2,1,0:T(8,128)(2,1)} %k_hbm.1, bf16[8,128,1024]{2,1,0:T(8,128)(2,1)} %v_hbm.1, s32[8,16]{1,0:T(8,128)} %bitcast.1, s32[16]{0:T(128)} %len_ref.1), custom_call_target="tpu_custom_call" | custom-call | tf_op jit(solution)/shard_map/pallas_call | solution.py:319
  24.0 1.3 %shard_map.69 = (bf16[16,512]{1,0:T(8,128)(2,1)}, f32[16,64]{1,0:T(8,128)}) custom-call(bf16[16,512]{1,0:T(8,128)(2,1)} %get-tuple-element.4.out_in, f32[16,64]{1,0:T(8,128)} %get-tuple-element.5.norm_in), custom_call_target="tpu_custom_call" | custom-call | tf_op jit(solution)/shard_map/pallas_call | solution.py:345

commit v3 on v2

--- a/solution.py
+++ b/solution.py
@@ -143,6 +143,8 @@
     st_stage,
     st_recv,
     e_rows,
+    w_rows,
+    t_rows,
     k_sem,
     v_sem,
     qs_sem,
@@ -233,7 +235,6 @@
     stat_lane = lax.broadcasted_iota(jnp.int32, (group, 128), 1)
     tops = [jnp.zeros((group, 128), jnp.float32) for _ in range(KVH)]
     sums = [jnp.ones((group, 128), jnp.float32) for _ in range(KVH)]
-    weights = {}
     for s in range(slots):
         k_copies[s].wait()
         is_valid = tok_lane < local_tok[:, s : s + 1]
@@ -251,23 +252,50 @@
             total = jnp.sum(expo, axis=1, keepdims=True)
             tops[k] = jnp.where(stat_lane == s, top, tops[k])
             sums[k] = jnp.where(stat_lane == s, total, sums[k])
-            weights[s, k] = (expo.astype(jnp.bfloat16), total)
+            w_rows[k, s * group : (s + 1) * group, :] = expo
+            t_rows[k, s * group : (s + 1) * group, :] = jnp.broadcast_to(1.0 / total, expo.shape)
     lse = jnp.concatenate(tops, axis=0) + jnp.log(jnp.concatenate(sums, axis=0))
     lse = jnp.concatenate([lse, jnp.zeros((128 - QH, 128), jnp.float32)], axis=0)
     st_stage[...] = jnp.transpose(lse)[:slots]
     st_copies = exchange(lambda dst: st_stage, st_recv, ss_sem, sr_sem)
     st_recv[me] = st_stage[...]
 
-    for s in range(slots):
-        v_copies[s].wait()
-        for k in range(KVH):
-            expo, total = weights[s, k]
+    for copy in v_copies:
+        copy.wait()
+    per = group // heads_dev
+    my_core = lax.rem(me, per)
+    middle = KVH // 2
+    order = [middle]
+    for away in range(middle - 1, 0, -1):
+        order += [away, KVH - away]
+    o_copies = []
+    for step in order + [0]:
+        k = lax.rem(me // per + step, KVH)
+        column = pl.multiple_of(k * HEAD, HEAD)
+        base = pl.multiple_of(k * group * slots, group * slots)
+        for s in range(slots):
+            rows = slice(s * group, (s + 1) * group)
             part = jnp.dot(
-                expo, v_vm[s, :, k * HEAD : (k + 1) * HEAD], preferred_element_type=jnp.float32
+                w_rows[k, rows, :].astype(jnp.bfloat16),
+                v_vm[s, :, pl.ds(column, HEAD)],
+                preferred_element_type=jnp.float32,
             )
-            o_rows[pl.ds(k * group * slots + s, group, stride=slots), :] = part / total
-    o_stage[...] = o_rows[...].reshape(n, heads_dev * slots, HEAD).astype(jnp.bfloat16)
-    o_copies = exchange(lambda dst: o_stage.at[dst], o_recv, os_sem, or_sem)
+            o_rows[pl.ds(base + s, group, stride=slots), :] = part * t_rows[k, rows, :]
+        done = o_rows[pl.ds(base, group * slots), :].astype(jnp.bfloat16)
+        o_stage[pl.ds(k * per, per)] = done.reshape(per, heads_dev * slots, HEAD)
+        for turn in range(per) if step else range(1, per):
+            dst = k * per + lax.rem(my_core + turn, per)
+            o_copies.append(
+                pltpu.make_async_remote_copy(
+                    src_ref=o_stage.at[dst],
+                    dst_ref=o_recv.at[me],
+                    send_sem=os_sem.at[step * per + turn],
+                    recv_sem=or_sem.at[step * per + turn],
+                    device_id={"seq": dst},
+                    device_id_type=pl.DeviceIdType.MESH,
+                )
+            )
+            o_copies[-1].start()
     o_recv[me] = o_stage[me]
 
     for copy in st_copies:
@@ -336,6 +364,8 @@
             pltpu.VMEM((slots, 128), jnp.float32),
             pltpu.VMEM((n, slots, 128), jnp.float32),
             pltpu.VMEM((128, n * slots), jnp.float32),
+            pltpu.VMEM((KVH, QH // KVH * slots, page_rows), jnp.float32),
+            pltpu.VMEM((KVH, QH // KVH * slots, page_rows), jnp.float32),
             pltpu.SemaphoreType.DMA((slots,)),
             pltpu.SemaphoreType.DMA((slots,)),
         ]
@@ -355,7 +385,8 @@
     slots, page_rows, _ = key_pages.shape
     whole_heads = queries.shape[1] % HEAD == 0
     whole_tiles = slots % 8 == 0 and (n * slots) % 128 == 0 and page_rows % 128 == 0
-    if whole_heads and whole_tiles and slots <= 128:
+    whole_tiles = whole_tiles and page_rows == HEAD
+    if whole_heads and whole_tiles and slots <= 128 and n % KVH == 0:
         return fused_body(n, queries, key_pages, value_pages, page_table, lengths)
     return generic_body(queries, key_pages, value_pages, page_table, lengths)
 

time: 25.7 us -> 26.4 us (1.027)
  Pallas kernels: 24.7 us -> 25.4 us
    pallas_call x1, Pallas kernels: 23.4 us -> 24.1 us  [fused_body(): pl.pallas_call(functools.partial(kernel, n), out_shape=(jax.ShapeDtypeStr...]
where the time goes in v3:
time: 26.4 us; the launch traced here: 26 us
  Pallas kernels  25.4 us (96%)
  between operations  0.64 us (2%)
    pallas_call x1, Pallas kernels, fused_body(): pl.pallas_call(functools.partial(kernel, n), out_shape=(jax.ShapeDtypeStr...  24.1 us
    pallas_call x1, Pallas kernels, fused_body(): pl.pallas_call(place, out_shape=tuple((jax.ShapeDtypeStruct(a.shape, a.dt...  1.33 us

profile of v3, /device:TPU:0, one launch (start us, length us, event | category | flops | bytes accessed | tf_op | source)
XLA Modules:
  0.0 26.0 jit_solution(2697674818058384573)
XLA Ops:
  0.6 24.1 %shard_map.68 = (bf16[16,512]{1,0:T(8,128)(2,1)}, f32[16,64]{1,0:T(8,128)}) custom-call(bf16[16,512]{1,0:T(8,128)(2,1)} %q_ref.1, bf16[8,128,1024]{2,1,0:T(8,128)(2,1)} %k_hbm.1, bf16[8,128,1024]{2,1,0:T(8,128)(2,1)} %v_hbm.1, s32[8,16]{1,0:T(8,128)} %bitcast.1, s32[16]{0:T(128)} %len_ref.1), custom_call_target="tpu_custom_call" | custom-call | tf_op jit(solution)/shard_map/pallas_call | solution.py:347
  24.7 1.3 %shard_map.69 = (bf16[16,512]{1,0:T(8,128)(2,1)}, f32[16,64]{1,0:T(8,128)}) custom-call(bf16[16,512]{1,0:T(8,128)(2,1)} %get-tuple-element.4.out_in, f32[16,64]{1,0:T(8,128)} %get-tuple-element.5.norm_in), custom_call_target="tpu_custom_call" | custom-call | tf_op jit(solution)/shard_map/pallas_call | solution.py:375
